TPU v7x, 256 devices: a whole 4x4x8 slice. The times are simulated.
256 devices in a mesh: comp: 32 (over z_lo, x, core), rows: 8 (over y, z_hi).
Axes of the slice: x: 4, y: 4, z: 8 (z_hi: 2, z_lo: 4; z = z_hi * 4 + z_lo), core: 2. Of those that a mesh axis runs over, the one named last changes fastest.
Arguments:
- hidden_states: bfloat16 [8, 2, 32, 128, 2560], P('rows', None, 'comp'), may hold values from -6 to 6
- queries: bfloat16 [8, 2, 32, 128, 1280], P('rows', None, 'comp'), may hold values from -900 to 900
- new_keys: bfloat16 [8, 2, 32, 128, 1280], P('rows', None, 'comp'), may hold values from -6 to 6
- new_values: bfloat16 [8, 2, 32, 128, 1280], P('rows', None, 'comp'), may hold values from -6 to 6
- out_grad: bfloat16 [8, 2, 32, 128, 1280], P('rows', None, 'comp'), may hold values from -6 to 6
- gate_weight: bfloat16 [2560, 128], replicated, may hold values from -0.125 to 0.125
- gate_bias: float32 [128], replicated, may hold values from -2 to 6
- prompt_state: float32 [8, 32, 2, 2, 2, 64, 640], P('rows', 'comp'), may hold values from -6 to 6
- owners: int32 [8, 2], P('rows'), may hold values from 0 to 31
- lengths: int32 [8, 2, 32], P('rows', None, 'comp'), may hold values from 32 to 128
- advantage: float32 [8, 2, 32], P('rows', None, 'comp'), may hold values from -4 to 4
Outputs:
- d_queries: bfloat16 [8, 2, 32, 128, 1280], P('rows', None, 'comp')
- d_keys: bfloat16 [8, 2, 32, 128, 1280], P('rows', None, 'comp')
- d_values: bfloat16 [8, 2, 32, 128, 1280], P('rows', None, 'comp')
- d_hidden: bfloat16 [8, 2, 32, 128, 2560], P('rows', None, 'comp')
- d_gate_weight: float32 [2560, 128], replicated
- d_gate_bias: float32 [128], replicated
- d_state: float32 [8, 2, 2, 2, 64, 640], P('rows', None, None, None, 'comp')
All inputs are finite; a program needn't handle non-finite values.
Results may differ from a plain program's by a relative error of at most 0.011.
Values sent between devices are 32-bit elements; how exact they have to be, the bound alone decides.
No kernel may reach another device: no remote copies, remote signals or barrier semaphores. Data moves between devices by JAX's collectives and lax.ppermute only.
A program may use at most 64 MiB of HBM per device.

v0:
```python
import jax
import jax.numpy as jnp
from jax import lax
from jax.sharding import PartitionSpec as P


def cut_along(value, dim, count):
    shape = value.shape
    blocks = value.reshape(*shape[:dim], count, shape[dim] // count, *shape[dim + 1 :])
    return jnp.moveaxis(blocks, dim, 0)


def sum_at_owner(value, axis, dim):
    count = lax.axis_size(axis)
    blocks = lax.all_to_all(cut_along(value, dim, count), axis, 0, 0, tiled=True)
    return jnp.sum(blocks, axis=0)


def slot_forward(gates, queries, keys_in, values_in, anchor_point):
    steps = queries.shape[0]
    heads = anchor_point.shape[1]
    slots = anchor_point.shape[2]
    width = anchor_point.shape[3]
    highest_score = lax.Precision.HIGHEST
    log_keep = jax.nn.log_sigmoid(gates).reshape(steps, heads, slots) / 8.0
    running = jnp.cumsum(log_keep, axis=0)
    inflow = -jnp.expm1(log_keep)
    places = jnp.arange(steps, dtype=jnp.int32)
    lower = (places[:, None] >= places[None, :])[:, :, None, None]
    between = running[:, None] - running[None, :]
    reach = jnp.where(lower, jnp.exp(jnp.where(lower, between, 0.0)), 0.0) * inflow[None]
    score_scale = width ** (-0.5)
    query_head_count = queries.astype(jnp.float32).reshape(steps, heads, width)
    key_heads = keys_in.astype(jnp.float32).reshape(steps, heads, width)
    value_heads = values_in.astype(jnp.float32).reshape(steps, heads, width)
    pairs = jnp.einsum("thd,jhd->thj", query_head_count, key_heads) * score_scale
    carried_state = jnp.exp(running)
    anchor_score_rows = (
        jnp.einsum("icv,crv->icr", query_head_count, anchor_point[0], precision=highest_score)
        * score_scale
    )
    scores = (
        jnp.einsum("tjhm,thj->thm", reach, pairs, precision=highest_score)
        + carried_state * anchor_score_rows
    )
    slot_probabilities = jax.nn.softmax(scores, axis=-1)
    mixing = jnp.einsum("thm,tjhm->thj", slot_probabilities, reach, precision=highest_score).astype(
        jnp.bfloat16
    )
    result_output = jnp.einsum("thj,jhd->thd", mixing.astype(jnp.float32), value_heads)
    result_output = result_output + jnp.einsum(
        "ivw,vwb->ivb", slot_probabilities * carried_state, anchor_point[1], precision=highest_score
    )
    return result_output.reshape(steps, heads * width)


def shards(
    hidden_states,
    queries,
    new_keys,
    new_values,
    out_grad,
    gate_weight,
    gate_bias,
    prompt_state,
    owners,
    lengths,
    advantage,
):
    local_states = prompt_state[0, 0]
    prompts = local_states.shape[0]
    steps = queries.shape[3]
    my_index = lax.axis_index("comp")
    owned = (owners[0] == my_index)[:, None, None, None, None]
    mine = jnp.where(owned, local_states, 0.0)
    pieces = sum_at_owner(mine, "comp", 3)
    anchors = lax.all_gather(pieces, "comp", axis=3, tiled=True)
    places = jnp.arange(steps, dtype=jnp.int32)
    sum_weight = jnp.zeros(gate_weight.shape, jnp.float32)
    sum_bias = jnp.zeros(gate_bias.shape, jnp.float32)
    state_terms = []
    out_q, out_k, out_v, out_x = ([], [], [], [])
    for prompt in range(prompts):
        list_q, list_k, list_v, list_x = ([], [], [], [])
        tokens = hidden_states[0, prompt, 0]
        gates = jnp.dot(tokens, gate_weight, preferred_element_type=jnp.float32) + gate_bias
        live = jnp.where(places < lengths[0, prompt, 0], 1.0, 0.0).astype(jnp.float32)
        cotangent = (advantage[0, prompt, 0] * live)[:, None] * out_grad[0, prompt, 0].astype(
            jnp.float32
        )
        result_output, pullback = jax.vjp(
            slot_forward,
            gates,
            queries[0, prompt, 0],
            new_keys[0, prompt, 0],
            new_values[0, prompt, 0],
            anchors[prompt],
        )
        grad_gates, grad_q, grad_k, grad_v, grad_anchor = pullback(cotangent)
        gates_low = grad_gates.astype(jnp.bfloat16)
        list_x.append(
            jnp.dot(gates_low, gate_weight.T, preferred_element_type=jnp.float32).astype(
                jnp.bfloat16
            )
        )
        sum_weight = sum_weight + jnp.dot(tokens.T, gates_low, preferred_element_type=jnp.float32)
        sum_bias = sum_bias + jnp.sum(grad_gates, axis=0)
        list_q.append(grad_q)
        list_k.append(grad_k)
        list_v.append(grad_v)
        state_terms.append(grad_anchor)
        out_q.append(jnp.stack(list_q))
        out_k.append(jnp.stack(list_k))
        out_v.append(jnp.stack(list_v))
        out_x.append(jnp.stack(list_x))
    state_grads = jnp.stack(state_terms)
    d_state = sum_at_owner(state_grads, "comp", 3)
    d_weight, d_bias = lax.psum((sum_weight, sum_bias), ("comp", "rows"))
    return (
        jnp.stack(out_q)[None],
        jnp.stack(out_k)[None],
        jnp.stack(out_v)[None],
        jnp.stack(out_x)[None],
        d_weight,
        d_bias,
        d_state[None],
    )


def solution(mesh):
    placed = (
        P("rows", None, "comp", None, None),
        P("rows", None, "comp", None, None),
        P("rows", None, "comp", None, None),
        P("rows", None, "comp", None, None),
        P("rows", None, "comp", None, None),
        P(),
        P(),
        P("rows", "comp", None, None, None, None, None),
        P("rows", None),
        P("rows", None, "comp"),
        P("rows", None, "comp"),
    )
    return jax.shard_map(
        shards,
        mesh=mesh,
        in_specs=placed,
        out_specs=(
            P("rows", None, "comp", None, None),
            P("rows", None, "comp", None, None),
            P("rows", None, "comp", None, None),
            P("rows", None, "comp", None, None),
            P(),
            P(),
            P("rows", None, None, None, "comp", None),
        ),
        check_vma=False,
    )
```

profile of v0, /device:TPU:2, one launch (start us, length us, event | category | flops | bytes accessed | tf_op | source)
XLA Modules:
  0.0 489.7 jit_solution(3050497754272828633)
XLA Ops:
  7.2 2.4 copy.282
  10.3 1.7 copy.283
  12.0 9.2 %all-to-all-start = ((f32[32,2,2,2,2,640]{5,4,3,2,1,0:T(2,128)}), f32[32,2,2,2,2,640]{5,4,3,2,1,0:T(2,128)S(1)}, u32[]{:S(2)}, u32[]{:S(2)}) async-start(f32[32,2,2,2,2,640]{5,4,3,2,1,0:T(2,128)} %copy.283), calls=%async_computation | async-start | bytes 2621440 | tf_op jit(solution)/shard_map/all_to_all | solution.py:15
  26.5 1.8 fusion.167
  32.5 1.7 copy.409
  37.3 11.7 %multiply_reduce_fusion.3 = (f32[128,2,64]{2,1,0:T(2,128)}, f32[128,2,64]{2,1,0:T(2,128)S(1)}) fusion(f32[128,2,128]{2,1,0:T(2,128)} %copy.407, f32[128,2,64]{0,2,1:T(8,128)S(1)} %exponential-minus-one_negate_fusion.1, f32[128,2,64]{0,2,1:T(8,128)S(1)} %copy.280, f32[128,2,64]{2,1,0:T(2,128)S(1)} %copy-done.35, pred[128,128]{1,0:T(8,128)(4,1)S(1)} %iota_compare_fusion, ...), kind=kLoop, calls=%fused_computation.5 | loop fusion | flops 25133056 | bytes 802816
  49.0 1.6 copy.355
  56.7 1.3 fusion.170
  58.0 1.3 fusion.169
  59.4 1.3 fusion.146
  60.7 1.3 bitcast_convert_fusion.5
  62.7 8.5 %fusion.10 = f32[128,2,1,64]{3,2,1,0:T(1,128)S(1)} fusion(f32[128,2,64]{0,2,1:T(8,128)S(1)} %copy-done.56, f32[128,2,64]{0,2,1:T(8,128)S(1)} %copy.280, f32[128,2,64]{2,1,0:T(2,128)S(1)} %copy-done.36, pred[128,128]{1,0:T(8,128)(4,1)S(1)} %iota_compare_fusion, bf16[128,2,128,1]{2,0,1,3:T(8,128)(2,1)S(1)} %bitcast.433), kind=kOutput, calls=%fused_computation.19 | convolution fusion | flops 33554432 | bytes 344064 | tf_op jit(solution)/shard_map/transpose(jvp(thm,tjhm->thj))/dot_general | solution.py:47
  71.5 1.3 fusion.147
  72.9 1.3 bitcast_convert_fusion.4
  74.9 8.7 %fusion.4 = f32[128,2,1,64]{3,2,1,0:T(1,128)S(1)} fusion(f32[128,2,64]{0,2,1:T(8,128)S(1)} %copy-done.52, f32[128,2,64]{0,2,1:T(8,128)S(1)} %copy.300, f32[128,2,64]{2,1,0:T(2,128)S(1)} %copy-done.32, pred[128,128]{1,0:T(8,128)(4,1)S(1)} %iota_compare_fusion, bf16[128,2,128,1]{2,0,1,3:T(8,128)(2,1)S(1)} %bitcast.434), kind=kOutput, calls=%fused_computation.14 | convolution fusion | flops 33554432 | bytes 344064 | tf_op jit(solution)/shard_map/transpose(jvp(thm,tjhm->thj))/dot_general | solution.py:47
  83.7 30.7 %all-gather.2.cloned.1.call-done = f32[2,2,2,64,640]{4,2,1,0,3:T(2,128)} async-done(((f32[2,2,2,2,640]{4,2,1,0,3:T(2,128)}), f32[2,2,2,64,640]{4,2,1,0,3:T(2,128)}) %all-gather.2.cloned.1.call-update) | async-done | bytes 1310736 | tf_op jit(solution)/shard_map/all_gather | solution.py:77
  114.4 2.5 fusion.164
  119.1 1.5 fusion.142
  121.3 1.6 convolution_bitcast_fusion.3
  125.2 1.6 fusion.84
  130.3 2.3 convolution_bitcast_fusion.1
  134.6 1.6 fusion.85
  138.9 11.8 %multiply_reduce_fusion.2 = (f32[128,2,128]{2,1,0:T(2,128)}, f32[128,2,128]{2,1,0:T(2,128)}) fusion(f32[128,2,64]{2,1,0:T(2,128)S(1)} %copy.408, f32[128,2,64]{0,2,1:T(8,128)} %copy-done.55, f32[128,2,64]{0,2,1:T(8,128)S(1)} %copy.280, f32[128,2,64]{2,1,0:T(2,128)} %fusion.171, pred[128,128]{1,0:T(8,128)(4,1)} %copy-done.59, f32[128,2,64]{0,2,1:T(8,128)} %copy-done.51, ...), kind=kLoop, calls=%fused_computation.4 | loop fusion | flops 25100288 | bytes 802816
  150.8 20.7 %fusion.13 = (f32[128,2,64]{0,2,1:T(8,128)}, f32[128,2,64]{2,1,0:T(2,128)}, f32[128,2,64]{0,2,1:T(8,128)}, f32[128,2,64]{0,2,1:T(8,128)}, f32[128,2,64]{2,1,0:T(2,128)}, /*index=5*/f32[128,2,64]{0,2,1:T(8,128)}) fusion(f32[128,2,64]{2,1,0:T(2,128)} %copy-done.44, f32[128,2,128]{2,1,0:T(2,128)S(1)} %copy-done.47, f32[128,2,64]{2,1,0:T(2,128)S(1)} %copy-done.42, ...), kind=kLoop, calls=%fused_computation.21 | loop fusion | flops 58621952 | bytes 1589248 | tf_op jit(solution)/shard_map/transpose(jvp())/reduce_sum | solution.py:30
  175.6 1.5 neg.93
  180.2 1.8 fusion.156
  183.2 1.4 fusion.61
  185.3 1.9 pad_add_fusion.1
  187.2 2.4 stack.25
  191.4 2.2 fusion.44
  194.5 1.9 copy.298
  199.3 1.5 stack.26
  200.8 1.9 copy.319
  202.6 1.7 copy_bitcast_fusion
  204.4 5.9 %all-to-all-start.1 = ((f32[32,2,2,2,2,640]{5,4,3,2,1,0:T(2,128)}), f32[32,2,2,2,2,640]{5,4,3,2,1,0:T(2,128)S(1)}, u32[]{:S(2)}, u32[]{:S(2)}) async-start(f32[32,2,2,2,2,640]{5,4,3,2,1,0:T(2,128)} %copy_bitcast_fusion), calls=%async_computation.1 | async-start | bytes 2621440 | tf_op jit(solution)/shard_map/all_to_all | solution.py:15
  210.7 2.2 fusion.43
  212.9 1.9 copy.315
  214.8 2.9 fusion.36
  217.8 2.0 maximum_bitcast_fusion.2
  220.8 8.3 %fusion.8 = bf16[128,2,1,128]{3,2,1,0:T(2,128)(2,1)S(1)} fusion(f32[128,2,64,1]{2,3,1,0:T(1,128)S(1)} %copy-done.41, f32[128,2,64]{0,2,1:T(8,128)S(1)} %copy-done.58, f32[128,2,64]{0,2,1:T(8,128)S(1)} %copy.280, f32[128,2,64]{2,1,0:T(2,128)S(1)} %copy-done.38, pred[128,128]{1,0:T(8,128)(4,1)S(1)} %copy-done.61), kind=kOutput, calls=%fused_computation.18 | convolution fusion | flops 33554432 | bytes 344064 | tf_op jit(solution)/shard_map/jvp(thm,tjhm->thj)/dot_general | solution.py:47
  230.1 8.4 %fusion.2 = bf16[128,2,1,128]{3,2,1,0:T(2,128)(2,1)S(1)} fusion(f32[128,2,64,1]{2,3,1,0:T(1,128)S(1)} %copy-done.40, f32[128,2,64]{0,2,1:T(8,128)S(1)} %copy-done.54, f32[128,2,64]{0,2,1:T(8,128)S(1)} %copy.300, f32[128,2,64]{2,1,0:T(2,128)S(1)} %copy-done.34, pred[128,128]{1,0:T(8,128)(4,1)S(1)} %copy-done.61), kind=kOutput, calls=%fused_computation.13 | convolution fusion | flops 33554432 | bytes 344064 | tf_op jit(solution)/shard_map/jvp(thm,tjhm->thj)/dot_general | solution.py:47
  239.9 1.9 copy.320
  241.8 1.9 copy.321
  244.8 2.2 copy.340
  247.0 77.3 %psum.15 = f32[128]{0:T(128)} all-reduce(f32[128]{0:T(128)S(1)} %negate_add_fusion), channel_id=1, replica_groups=mesh['comp'=32,'rows'=8] {'comp','rows'}, use_global_device_ids=true, to_apply=%region_20.22 | all-reduce | flops 128 | bytes 1024 | tf_op jit(solution)/shard_map/psum | solution.py:118
  324.3 2.0 maximum_bitcast_fusion.3
  327.5 151.4 %all-reduce.6.cloned.1.call-done = f32[2560,128]{0,1:T(8,128)} async-done(((f32[2560,128]{0,1:T(8,128)}), f32[2560,128]{0,1:T(8,128)}) %all-reduce.6.cloned.1.call-update) | async-done | bytes 1310736 | tf_op jit(solution)/shard_map/psum | solution.py:118
  478.8 2.8 copy.343
  (231 shorter events, 56.3 us)
Async XLA Ops:
  7.2 14.6 %copy-start = (bf16[2560,128]{1,0:T(8,128)(2,1)S(1)}, bf16[2560,128]{1,0:T(8,128)(2,1)}, u32[]{:S(2)}) copy-start(bf16[2560,128]{1,0:T(8,128)(2,1)} %param.17) | copy-start | bytes 1966084
  12.0 9.8 %copy-start.11 = (bf16[1,2,1,128,2560]{4,3,2,1,0:T(8,128)(2,1)S(1)}, bf16[1,2,1,128,2560]{4,3,2,1,0:T(8,128)(2,1)}, u32[]{:S(2)}) copy-start(bf16[1,2,1,128,2560]{4,3,2,1,0:T(8,128)(2,1)} %param.12) | copy-start | bytes 3932164
  12.0 9.8 %copy-start.71 = (f32[128]{0:T(128)S(1)}, f32[128]{0:T(128)}, u32[]{:S(2)}) copy-start(f32[128]{0:T(128)} %param.18) | copy-start | bytes 1540
  12.0 42.2 %all-to-all-start = ((f32[32,2,2,2,2,640]{5,4,3,2,1,0:T(2,128)}), f32[32,2,2,2,2,640]{5,4,3,2,1,0:T(2,128)S(1)}, u32[]{:S(2)}, u32[]{:S(2)}) async-start(f32[32,2,2,2,2,640]{5,4,3,2,1,0:T(2,128)} %copy.283), calls=%async_computation | async-start | bytes 2621440 | tf_op jit(solution)/shard_map/all_to_all | solution.py:15
  21.2 93.2 %all-gather.2.cloned.1.call-start = ((), (), s32[]{:S(2)}) async-start(), calls=%async_computation.2 | async-start | bytes 1351680 | tf_op jit(solution)/shard_map/all_gather | solution.py:77
  24.1 13.2 %copy-start.31 = (f32[128,2,64]{2,1,0:T(2,128)}, f32[128,2,64]{2,1,0:T(2,128)S(1)}, u32[]{:S(2)}) copy-start(f32[128,2,64]{2,1,0:T(2,128)S(1)} %fusion.172) | copy-start | bytes 196612
  34.4 14.6 %copy-start.2 = (bf16[1,1,1,128,1280]{3,4,2,1,0:T(8,128)(2,1)}, bf16[1,1,1,128,1280]{3,4,2,1,0:T(8,128)(2,1)S(1)}, u32[]{:S(2)}) copy-start(bf16[1,1,1,128,1280]{3,4,2,1,0:T(8,128)(2,1)S(1)} %copy.399) | copy-start | bytes 983044
  35.5 39.4 %copy-start.59 = (pred[128,128]{1,0:T(8,128)(4,1)}, pred[128,128]{1,0:T(8,128)(4,1)S(1)}, u32[]{:S(2)}) copy-start(pred[128,128]{1,0:T(8,128)(4,1)S(1)} %iota_compare_fusion) | copy-start | bytes 49156
  36.4 12.6 %copy-start.51 = (f32[128,2,64]{0,2,1:T(8,128)}, f32[128,2,64]{0,2,1:T(8,128)S(1)}, u32[]{:S(2)}) copy-start(f32[128,2,64]{0,2,1:T(8,128)S(1)} %exponential-minus-one_negate_fusion) | copy-start | bytes 196612
  37.3 11.7 %copy-start.55 = (f32[128,2,64]{0,2,1:T(8,128)}, f32[128,2,64]{0,2,1:T(8,128)S(1)}, u32[]{:S(2)}) copy-start(f32[128,2,64]{0,2,1:T(8,128)S(1)} %exponential-minus-one_negate_fusion.1) | copy-start | bytes 196612
  56.5 6.2 %copy-start.36 = (f32[128,2,64]{2,1,0:T(2,128)S(1)}, f32[128,2,64]{2,1,0:T(2,128)}, u32[]{:S(2)}) copy-start(f32[128,2,64]{2,1,0:T(2,128)} %fusion.171) | copy-start | bytes 196612
  56.7 6.0 %copy-start.56 = (f32[128,2,64]{0,2,1:T(8,128)S(1)}, f32[128,2,64]{0,2,1:T(8,128)}, u32[]{:S(2)}) copy-start(f32[128,2,64]{0,2,1:T(8,128)} %copy-done.55) | copy-start | bytes 196612
  60.6 10.5 %copy-start.64 = (f32[128]{0:T(128)}, f32[128]{0:T(128)S(1)}, u32[]{:S(2)}) copy-start(f32[128]{0:T(128)S(1)} %fusion.146) | copy-start | bytes 1540
  71.3 46.6 %copy-start.7 = (f32[128,2,1,64]{0,3,1,2:T(8,128)}, f32[128,2,1,64]{0,3,1,2:T(8,128)S(1)}, u32[]{:S(2)}) copy-start(f32[128,2,1,64]{0,3,1,2:T(8,128)S(1)} %copy.347) | copy-start | bytes 196612
  72.8 10.7 %copy-start.67 = (f32[128]{0:T(128)}, f32[128]{0:T(128)S(1)}, u32[]{:S(2)}) copy-start(f32[128]{0:T(128)S(1)} %fusion.147) | copy-start | bytes 1540
  83.7 34.2 %copy-start.65 = (f32[128]{0:T(128)S(1)}, f32[128]{0:T(128)}, u32[]{:S(2)}) copy-start(f32[128]{0:T(128)} %copy-done.64) | copy-start | bytes 1540
  119.1 6.2 %copy-start.62 = (f32[128,2]{0,1:T(2,128)}, f32[128,2]{0,1:T(2,128)S(1)}, u32[]{:S(2)}) copy-start(f32[128,2]{0,1:T(2,128)S(1)} %get-tuple-element.95) | copy-start | bytes 3076
  127.1 5.5 %copy-start.28 = (f32[2,64,128]{2,1,0:T(8,128)}, f32[2,64,128]{2,1,0:T(8,128)S(1)}, u32[]{:S(2)}) copy-start(f32[2,64,128]{2,1,0:T(8,128)S(1)} %get-tuple-element.109) | copy-start | bytes 196612
  127.2 5.4 %copy-start.25 = (f32[128,2,64]{0,2,1:T(8,128)S(1)}, f32[128,2,64]{0,2,1:T(8,128)}, u32[]{:S(2)}) copy-start(f32[128,2,64]{0,2,1:T(8,128)} %copy.376) | copy-start | bytes 196612
  127.8 6.8 %copy-start.22 = (f32[2,128,64]{1,2,0:T(8,128)}, f32[2,128,64]{1,2,0:T(8,128)S(1)}, u32[]{:S(2)}) copy-start(f32[2,128,64]{1,2,0:T(8,128)S(1)} %get-tuple-element.111) | copy-start | bytes 196612
  138.8 11.9 %copy-start.33 = (f32[128,2,64]{2,1,0:T(2,128)S(1)}, f32[128,2,64]{2,1,0:T(2,128)}, u32[]{:S(2)}) copy-start(f32[128,2,64]{2,1,0:T(2,128)} %copy-done.31) | copy-start | bytes 196612
  138.8 11.9 %copy-start.37 = (f32[128,2,64]{2,1,0:T(2,128)S(1)}, f32[128,2,64]{2,1,0:T(2,128)}, u32[]{:S(2)}) copy-start(f32[128,2,64]{2,1,0:T(2,128)} %fusion.171) | copy-start | bytes 196612
  138.8 11.9 %copy-start.42 = (f32[128,2,64]{2,1,0:T(2,128)S(1)}, f32[128,2,64]{2,1,0:T(2,128)}, u32[]{:S(2)}) copy-start(f32[128,2,64]{2,1,0:T(2,128)} %copy.323) | copy-start | bytes 196612
  138.8 11.9 %copy-start.43 = (f32[128,2,64]{2,1,0:T(2,128)S(1)}, f32[128,2,64]{2,1,0:T(2,128)}, u32[]{:S(2)}) copy-start(f32[128,2,64]{2,1,0:T(2,128)} %copy.330) | copy-start | bytes 196612
  138.8 11.9 %copy-start.46 = (f32[128,2,128]{2,1,0:T(2,128)S(1)}, f32[128,2,128]{2,1,0:T(2,128)}, u32[]{:S(2)}) copy-start(f32[128,2,128]{2,1,0:T(2,128)} %copy.409) | copy-start | bytes 393220
  138.8 11.9 %copy-start.47 = (f32[128,2,128]{2,1,0:T(2,128)S(1)}, f32[128,2,128]{2,1,0:T(2,128)}, u32[]{:S(2)}) copy-start(f32[128,2,128]{2,1,0:T(2,128)} %copy.407) | copy-start | bytes 393220
  138.8 11.9 %copy-start.48 = (f32[128,2,128]{2,1,0:T(2,128)S(1)}, f32[128,2,128]{2,1,0:T(2,128)}, u32[]{:S(2)}) copy-start(f32[128,2,128]{2,1,0:T(2,128)} %copy.322) | copy-start | bytes 393220
  138.8 11.9 %copy-start.49 = (f32[128,2,128]{2,1,0:T(2,128)S(1)}, f32[128,2,128]{2,1,0:T(2,128)}, u32[]{:S(2)}) copy-start(f32[128,2,128]{2,1,0:T(2,128)} %copy.329) | copy-start | bytes 393220
  138.8 11.9 %copy-start.53 = (f32[128,2,64]{0,2,1:T(8,128)S(1)}, f32[128,2,64]{0,2,1:T(8,128)}, u32[]{:S(2)}) copy-start(f32[128,2,64]{0,2,1:T(8,128)} %copy-done.51) | copy-start | bytes 196612
  138.9 11.9 %copy-start.57 = (f32[128,2,64]{0,2,1:T(8,128)S(1)}, f32[128,2,64]{0,2,1:T(8,128)}, u32[]{:S(2)}) copy-start(f32[128,2,64]{0,2,1:T(8,128)} %copy-done.55) | copy-start | bytes 196612
  138.9 11.9 %copy-start.60 = (pred[128,128]{1,0:T(8,128)(4,1)S(1)}, pred[128,128]{1,0:T(8,128)(4,1)}, u32[]{:S(2)}) copy-start(pred[128,128]{1,0:T(8,128)(4,1)} %copy-done.59) | copy-start | bytes 49156
  150.7 21.7 %copy-start.8 = (f32[128,2,1,64]{0,3,1,2:T(8,128)S(1)}, f32[128,2,1,64]{0,3,1,2:T(8,128)}, u32[]{:S(2)}) copy-start(f32[128,2,1,64]{0,3,1,2:T(8,128)} %copy-done.7) | copy-start | bytes 196612
  150.7 21.7 %copy-start.10 = (f32[128,2,64]{0,2,1:T(8,128)S(1)}, f32[128,2,64]{0,2,1:T(8,128)}, u32[]{:S(2)}) copy-start(f32[128,2,64]{0,2,1:T(8,128)} %copy-done.9) | copy-start | bytes 196612
  150.7 21.7 %copy-start.21 = (f32[2,128,64]{1,2,0:T(8,128)S(1)}, f32[2,128,64]{1,2,0:T(8,128)}, u32[]{:S(2)}) copy-start(f32[2,128,64]{1,2,0:T(8,128)} %copy-done.20) | copy-start | bytes 196612
  150.8 21.7 %copy-start.27 = (f32[2,64,128]{2,1,0:T(8,128)S(1)}, f32[2,64,128]{2,1,0:T(8,128)}, u32[]{:S(2)}) copy-start(f32[2,64,128]{2,1,0:T(8,128)} %get-tuple-element.106) | copy-start | bytes 196612
  171.4 6.6 %copy-start.23 = (f32[2,128,64]{1,2,0:T(8,128)S(1)}, f32[2,128,64]{1,2,0:T(8,128)}, u32[]{:S(2)}) copy-start(f32[2,128,64]{1,2,0:T(8,128)} %copy-done.22) | copy-start | bytes 196612
  171.4 6.6 %copy-start.29 = (f32[2,64,128]{2,1,0:T(8,128)S(1)}, f32[2,64,128]{2,1,0:T(8,128)}, u32[]{:S(2)}) copy-start(f32[2,64,128]{2,1,0:T(8,128)} %copy-done.28) | copy-start | bytes 196612
  185.3 5.0 %copy-start.50 = (f32[128,2,128]{2,1,0:T(2,128)S(1)}, f32[128,2,128]{2,1,0:T(2,128)}, u32[]{:S(2)}) copy-start(f32[128,2,128]{2,1,0:T(2,128)} %get-tuple-element.66) | copy-start | bytes 393220
  193.6 4.8 copy-start.17
  204.4 277.2 %all-to-all-start.1 = ((f32[32,2,2,2,2,640]{5,4,3,2,1,0:T(2,128)}), f32[32,2,2,2,2,640]{5,4,3,2,1,0:T(2,128)S(1)}, u32[]{:S(2)}, u32[]{:S(2)}) async-start(f32[32,2,2,2,2,640]{5,4,3,2,1,0:T(2,128)} %copy_bitcast_fusion), calls=%async_computation.1 | async-start | bytes 2621440 | tf_op jit(solution)/shard_map/all_to_all | solution.py:15
  210.3 268.6 %all-reduce.6.cloned.1.call-start = ((), (), s32[]{:S(2)}) async-start(), calls=%async_computation.3 | async-start | bytes 2621440 | tf_op jit(solution)/shard_map/psum | solution.py:118
  220.8 8.3 %copy-start.66 = (f32[128]{0:T(128)S(1)}, f32[128]{0:T(128)}, u32[]{:S(2)}) copy-start(f32[128]{0:T(128)} %copy-done.64) | copy-start | bytes 1540
  220.8 9.3 %copy-start.34 = (f32[128,2,64]{2,1,0:T(2,128)S(1)}, f32[128,2,64]{2,1,0:T(2,128)}, u32[]{:S(2)}) copy-start(f32[128,2,64]{2,1,0:T(2,128)} %copy-done.31) | copy-start | bytes 196612
  220.8 9.3 %copy-start.40 = (f32[128,2,64,1]{2,3,1,0:T(1,128)S(1)}, f32[128,2,64,1]{2,3,1,0:T(1,128)}, u32[]{:S(2)}) copy-start(f32[128,2,64,1]{2,3,1,0:T(1,128)} %copy.390) | copy-start | bytes 196612
  220.8 9.3 %copy-start.54 = (f32[128,2,64]{0,2,1:T(8,128)S(1)}, f32[128,2,64]{0,2,1:T(8,128)}, u32[]{:S(2)}) copy-start(f32[128,2,64]{0,2,1:T(8,128)} %copy-done.51) | copy-start | bytes 196612
  230.1 8.5 %copy-start.69 = (f32[128]{0:T(128)S(1)}, f32[128]{0:T(128)}, u32[]{:S(2)}) copy-start(f32[128]{0:T(128)} %copy-done.67) | copy-start | bytes 1540
  230.1 9.4 %copy-start.30 = (f32[128,128]{0,1:T(8,128)S(1)}, f32[128,128]{0,1:T(8,128)}, u32[]{:S(2)}) copy-start(f32[128,128]{0,1:T(8,128)} %get-tuple-element.117) | copy-start | bytes 196612
  244.8 81.5 %copy-start.4 = (bf16[1,1,128,2560]{3,2,1,0:T(8,128)(2,1)S(1)}, bf16[1,1,128,2560]{3,2,1,0:T(8,128)(2,1)}, u32[]{:S(2)}) copy-start(bf16[1,1,128,2560]{3,2,1,0:T(8,128)(2,1)} %fusion.37) | copy-start | bytes 1966084
  (28 other events, 75.6 us)
Sparse Core Ops, SparseCore 0:
  55.4 58.9 all-gather.1
  217.9 260.9 all-reduce.5
where the time goes:
time: 494 us; the launch traced here: 490 us
  waiting for transfers between devices  182 us (37%)
  blocking collectives  77.3 us (16%)
  other arithmetic  76.5 us (15%)
  matrix products  65.9 us (13%)
  local copies, waits for them, and re-layouts  56.7 us (11%)
  starting transfers between devices  16.1 us (3%)
  between operations  15.1 us (3%)
    psum x1, waiting for transfers between devices, shards(): d_weight, d_bias = lax.psum((sum_weight, sum_bias), ('comp', 'rows'))  151 us
    psum x1, blocking collectives, shards(): d_weight, d_bias = lax.psum((sum_weight, sum_bias), ('comp', 'rows'))  77.3 us
    dot_general x4, matrix products, slot_forward(): jnp.einsum('thm,tjhm->thj', slot_probabilities, reach, precision=highest_...  33.9 us
    all_gather x1, waiting for transfers between devices, shards(): anchors = lax.all_gather(pieces, 'comp', axis=3, tiled=True)  30.7 us
    unnamed x3, other arithmetic  24.6 us
    reduce_sum x1, other arithmetic, slot_forward(): between = running[:, None] - running[None, :]  20.7 us
    unnamed x158, local copies, waits for them, and re-layouts  18 us
    all_to_all x2, starting transfers between devices, sum_at_owner(): lax.all_to_all(cut_along(value, dim, count), axis, 0, 0, tiled=True)  15.1 us
  transfers between devices with their start and end apart: 4, of which 2 were waited for; matrix products, arithmetic and copies ran while one was open for 21% of the time, Pallas kernels for 0%

commit v1 on v0

--- a/solution.py
+++ b/solution.py
@@ -115,7 +115,7 @@
         out_x.append(jnp.stack(list_x))
     state_grads = jnp.stack(state_terms)
     d_state = sum_at_owner(state_grads, "comp", 3)
-    d_weight, d_bias = lax.psum((sum_weight, sum_bias), ("comp", "rows"))
+    d_weight, d_bias = lax.psum(lax.psum((sum_weight, sum_bias), "rows"), "comp")
     return (
         jnp.stack(out_q)[None],
         jnp.stack(out_k)[None],

time: 494 us -> 669 us (1.35)
  the two profiles are of different devices: /device:TPU:2 before, /device:TPU:1 now
where the time goes in v1:
time: 669 us; the launch traced here: 662 us
  waiting for transfers between devices  349 us (52%)
  blocking collectives  97.8 us (15%)
  other arithmetic  71 us (11%)
  matrix products  64.9 us (10%)
  local copies, waits for them, and re-layouts  48.6 us (7%)
  starting transfers between devices  15.7 us (2%)
  between operations  15 us (2%)
    psum x1, waiting for transfers between devices, shards(): lax.psum(lax.psum((sum_weight, sum_bias), 'rows'), 'comp')  179 us
    psum x1, waiting for transfers between devices, shards(): lax.psum((sum_weight, sum_bias), 'rows')  139 us
    psum x1, blocking collectives, shards(): lax.psum(lax.psum((sum_weight, sum_bias), 'rows'), 'comp')  74.9 us
    dot_general x4, matrix products, slot_forward(): jnp.einsum('thm,tjhm->thj', slot_probabilities, reach, precision=highest_...  36.4 us
    all_gather x1, waiting for transfers between devices, shards(): anchors = lax.all_gather(pieces, 'comp', axis=3, tiled=True)  31.3 us
    unnamed x3, other arithmetic  23.6 us
    psum x1, blocking collectives, shards(): lax.psum((sum_weight, sum_bias), 'rows')  22.9 us
    reduce_sum x1, other arithmetic, slot_forward(): between = running[:, None] - running[None, :]  19.5 us
  transfers between devices with their start and end apart: 5, of which 3 were waited for; matrix products, arithmetic and copies ran while one was open for 12% of the time, Pallas kernels for 0%

profile of v1, /device:TPU:1, one launch (start us, length us, event | category | flops | bytes accessed | tf_op | source)
XLA Modules:
  0.0 661.8 jit_solution(1098314084651012816)
XLA Ops:
  7.2 2.4 copy.282
  10.3 1.7 copy.283
  12.0 10.1 %all-to-all-start = ((f32[32,2,2,2,2,640]{5,4,3,2,1,0:T(2,128)}), f32[32,2,2,2,2,640]{5,4,3,2,1,0:T(2,128)S(1)}, u32[]{:S(2)}, u32[]{:S(2)}) async-start(f32[32,2,2,2,2,640]{5,4,3,2,1,0:T(2,128)} %copy.283), calls=%async_computation | async-start | bytes 2621440 | tf_op jit(solution)/shard_map/all_to_all | solution.py:15
  22.2 2.2 negate_multiply_fusion
  27.2 1.8 fusion.167
  31.2 1.7 copy.409
  37.0 11.7 %multiply_reduce_fusion.3 = (f32[128,2,64]{2,1,0:T(2,128)}, f32[128,2,64]{2,1,0:T(2,128)S(1)}) fusion(f32[128,2,128]{2,1,0:T(2,128)} %copy.407, f32[128,2,64]{0,2,1:T(8,128)S(1)} %exponential-minus-one_negate_fusion.1, f32[128,2,64]{0,2,1:T(8,128)S(1)} %copy.280, f32[128,2,64]{2,1,0:T(2,128)S(1)} %copy-done.38, pred[128,128]{1,0:T(8,128)(4,1)S(1)} %iota_compare_fusion, ...), kind=kLoop, calls=%fused_computation.5 | loop fusion | flops 25133056 | bytes 802816
  48.7 1.6 copy.355
  56.6 1.3 fusion.170
  57.9 1.3 fusion.169
  60.5 1.3 bitcast_convert_fusion.5
  62.5 8.5 %fusion.10 = f32[128,2,1,64]{3,2,1,0:T(1,128)S(1)} fusion(f32[128,2,64]{0,2,1:T(8,128)S(1)} %copy-done.63, f32[128,2,64]{0,2,1:T(8,128)S(1)} %copy.280, f32[128,2,64]{2,1,0:T(2,128)S(1)} %copy-done.39, pred[128,128]{1,0:T(8,128)(4,1)S(1)} %iota_compare_fusion, bf16[128,2,128,1]{2,0,1,3:T(8,128)(2,1)S(1)} %bitcast.433), kind=kOutput, calls=%fused_computation.19 | convolution fusion | flops 33554432 | bytes 344064 | tf_op jit(solution)/shard_map/transpose(jvp(thm,tjhm->thj))/dot_general | solution.py:47
  71.4 1.3 fusion.147
  72.7 1.3 bitcast_convert_fusion.4
  74.8 8.5 %fusion.4 = f32[128,2,1,64]{3,2,1,0:T(1,128)S(1)} fusion(f32[128,2,64]{0,2,1:T(8,128)S(1)} %copy-done.58, f32[128,2,64]{0,2,1:T(8,128)S(1)} %copy.300, f32[128,2,64]{2,1,0:T(2,128)S(1)} %copy-done.33, pred[128,128]{1,0:T(8,128)(4,1)S(1)} %iota_compare_fusion, bf16[128,2,128,1]{2,0,1,3:T(8,128)(2,1)S(1)} %bitcast.434), kind=kOutput, calls=%fused_computation.14 | convolution fusion | flops 33554432 | bytes 344064 | tf_op jit(solution)/shard_map/transpose(jvp(thm,tjhm->thj))/dot_general | solution.py:47
  83.4 31.3 %all-gather.2.cloned.1.call-done = f32[2,2,2,64,640]{4,2,1,0,3:T(2,128)} async-done(((f32[2,2,2,2,640]{4,2,1,0,3:T(2,128)}), f32[2,2,2,64,640]{4,2,1,0,3:T(2,128)}) %all-gather.2.cloned.1.call-update) | async-done | bytes 1310736 | tf_op jit(solution)/shard_map/all_gather | solution.py:77
  114.7 2.5 fusion.164
  119.4 1.5 fusion.142
  121.7 1.6 convolution_bitcast_fusion.3
  124.3 1.2 convolution_bitcast_fusion.2
  125.5 1.6 fusion.84
  129.3 1.5 fusion.144
  131.6 1.6 convolution_bitcast_fusion.1
  134.7 9.7 %fusion.8 = bf16[128,2,1,128]{3,2,1,0:T(2,128)(2,1)S(1)} fusion(f32[128,2,64,1]{2,3,1,0:T(1,128)} %copy.388, f32[128,2,64]{0,2,1:T(8,128)} %copy-done.62, f32[128,2,64]{0,2,1:T(8,128)S(1)} %copy.280, f32[128,2,64]{2,1,0:T(2,128)} %copy-done.37, pred[128,128]{1,0:T(8,128)(4,1)} %copy-done.66), kind=kOutput, calls=%fused_computation.18 | convolution fusion | flops 33554432 | bytes 344064 | tf_op jit(solution)/shard_map/jvp(thm,tjhm->thj)/dot_general | solution.py:47
  146.3 1.5 stack.25
  148.7 9.7 %fusion.2 = bf16[128,2,1,128]{3,2,1,0:T(2,128)(2,1)} fusion(f32[128,2,64,1]{2,3,1,0:T(1,128)S(1)} %copy.390, f32[128,2,64]{0,2,1:T(8,128)S(1)} %copy-done.59, f32[128,2,64]{0,2,1:T(8,128)S(1)} %copy.300, f32[128,2,64]{2,1,0:T(2,128)S(1)} %copy-done.34, pred[128,128]{1,0:T(8,128)(4,1)} %copy-done.66), kind=kOutput, calls=%fused_computation.13 | convolution fusion | flops 33554432 | bytes 344064 | tf_op jit(solution)/shard_map/jvp(thm,tjhm->thj)/dot_general | solution.py:47
  158.5 10.7 %multiply_reduce_fusion.2 = (f32[128,2,128]{2,1,0:T(2,128)}, f32[128,2,128]{2,1,0:T(2,128)}) fusion(f32[128,2,64]{2,1,0:T(2,128)S(1)} %copy-done.48, f32[128,2,64]{0,2,1:T(8,128)S(1)} %copy-done.64, f32[128,2,64]{0,2,1:T(8,128)S(1)} %copy.280, f32[128,2,64]{2,1,0:T(2,128)S(1)} %copy-done.40, pred[128,128]{1,0:T(8,128)(4,1)S(1)} %copy-done.67, ...), kind=kLoop, calls=%fused_computation.4 | loop fusion | flops 25100288 | bytes 802816
  169.2 1.7 copy.362
  171.0 2.1 fusion.41
  173.0 2.2 fusion.44
  175.4 19.5 %fusion.13 = (f32[128,2,64]{0,2,1:T(8,128)}, f32[128,2,64]{2,1,0:T(2,128)S(1)}, f32[128,2,64]{0,2,1:T(8,128)}, f32[128,2,64]{0,2,1:T(8,128)}, f32[128,2,64]{2,1,0:T(2,128)}, /*index=5*/f32[128,2,64]{0,2,1:T(8,128)}) fusion(f32[128,2,64]{2,1,0:T(2,128)S(1)} %copy-done.49, f32[128,2,128]{2,1,0:T(2,128)S(1)} %copy-done.53, f32[128,2,64]{2,1,0:T(2,128)S(1)} %copy-done.46, ...), kind=kLoop, calls=%fused_computation.21 | loop fusion | flops 58621952 | bytes 1589248 | tf_op jit(solution)/shard_map/transpose(jvp())/reduce_sum | solution.py:30
  197.3 1.5 neg.88
  198.8 1.5 neg.93
  206.5 1.5 stack.26
  208.0 1.3 fusion.156
  209.3 1.4 fusion.61
  210.7 1.4 fusion.36
  212.1 1.7 copy_bitcast_fusion
  213.8 1.9 copy.320
  215.8 1.9 copy.317
  218.7 5.3 all-to-all-start.1
  224.0 1.9 convolution_convert_fusion.4
  225.9 1.9 copy.321
  231.7 138.5 %all-reduce.7.cloned.1.call-done = f32[2560,128]{0,1:T(8,128)} async-done(((f32[2560,128]{0,1:T(8,128)}), f32[2560,128]{0,1:T(8,128)}) %all-reduce.7.cloned.1.call-update) | async-done | bytes 1310736 | tf_op jit(solution)/shard_map/psum | solution.py:118
  371.4 22.9 %psum.30 = f32[128]{0:T(128)S(1)} all-reduce(f32[128]{0:T(128)S(1)} %negate_add_fusion), channel_id=1, replica_groups=mesh['comp'=32,'rows'=8] {'rows'}, use_global_device_ids=true, to_apply=%region_21.23 | all-reduce | flops 128 | bytes 1024 | tf_op jit(solution)/shard_map/psum | solution.py:118
  394.3 74.9 %psum.31 = f32[128]{0:T(128)} all-reduce(f32[128]{0:T(128)S(1)} %psum.30), channel_id=1, replica_groups=mesh['comp'=32,'rows'=8] {'comp'}, use_global_device_ids=true, to_apply=%region_22.24 | all-reduce | flops 128 | bytes 1024 | tf_op jit(solution)/shard_map/psum | solution.py:118
  473.4 179.0 %all-reduce.9.cloned.1.call-done = f32[2560,128]{0,1:T(8,128)} async-done(((f32[2560,128]{0,1:T(8,128)}), f32[2560,128]{0,1:T(8,128)}) %all-reduce.9.cloned.1.call-update) | async-done | bytes 1310736 | tf_op jit(solution)/shard_map/psum | solution.py:118
  652.3 2.8 copy.343
  (251 shorter events, 49.1 us)
Async XLA Ops:
  7.2 15.0 %copy-start = (bf16[2560,128]{1,0:T(8,128)(2,1)S(1)}, bf16[2560,128]{1,0:T(8,128)(2,1)}, u32[]{:S(2)}) copy-start(bf16[2560,128]{1,0:T(8,128)(2,1)} %param.17) | copy-start | bytes 1966084
  12.0 10.2 %copy-start.79 = (f32[128]{0:T(128)S(1)}, f32[128]{0:T(128)}, u32[]{:S(2)}) copy-start(f32[128]{0:T(128)} %param.18) | copy-start | bytes 1540
  12.0 41.9 %all-to-all-start = ((f32[32,2,2,2,2,640]{5,4,3,2,1,0:T(2,128)}), f32[32,2,2,2,2,640]{5,4,3,2,1,0:T(2,128)S(1)}, u32[]{:S(2)}, u32[]{:S(2)}) async-start(f32[32,2,2,2,2,640]{5,4,3,2,1,0:T(2,128)} %copy.283), calls=%async_computation | async-start | bytes 2621440 | tf_op jit(solution)/shard_map/all_to_all | solution.py:15
  22.2 92.6 %all-gather.2.cloned.1.call-start = ((), (), s32[]{:S(2)}) async-start(), calls=%async_computation.2 | async-start | bytes 1351680 | tf_op jit(solution)/shard_map/all_gather | solution.py:77
  25.7 11.2 %copy-start.32 = (f32[128,2,64]{2,1,0:T(2,128)}, f32[128,2,64]{2,1,0:T(2,128)S(1)}, u32[]{:S(2)}) copy-start(f32[128,2,64]{2,1,0:T(2,128)S(1)} %fusion.172) | copy-start | bytes 196612
  29.2 4.8 copy-start.1
  34.1 14.6 %copy-start.3 = (bf16[1,1,1,128,1280]{3,4,2,1,0:T(8,128)(2,1)}, bf16[1,1,1,128,1280]{3,4,2,1,0:T(8,128)(2,1)S(1)}, u32[]{:S(2)}) copy-start(bf16[1,1,1,128,1280]{3,4,2,1,0:T(8,128)(2,1)S(1)} %copy.399) | copy-start | bytes 983044
  35.2 39.6 %copy-start.66 = (pred[128,128]{1,0:T(8,128)(4,1)}, pred[128,128]{1,0:T(8,128)(4,1)S(1)}, u32[]{:S(2)}) copy-start(pred[128,128]{1,0:T(8,128)(4,1)S(1)} %iota_compare_fusion) | copy-start | bytes 49156
  36.0 12.6 %copy-start.57 = (f32[128,2,64]{0,2,1:T(8,128)}, f32[128,2,64]{0,2,1:T(8,128)S(1)}, u32[]{:S(2)}) copy-start(f32[128,2,64]{0,2,1:T(8,128)S(1)} %exponential-minus-one_negate_fusion) | copy-start | bytes 196612
  37.0 11.7 %copy-start.62 = (f32[128,2,64]{0,2,1:T(8,128)}, f32[128,2,64]{0,2,1:T(8,128)S(1)}, u32[]{:S(2)}) copy-start(f32[128,2,64]{0,2,1:T(8,128)S(1)} %exponential-minus-one_negate_fusion.1) | copy-start | bytes 196612
  55.0 315.2 %all-reduce.7.cloned.1.call-start = ((), (), s32[]{:S(2)}) async-start(), calls=%async_computation.3 | async-start | bytes 2621440 | tf_op jit(solution)/shard_map/psum | solution.py:118
  56.4 6.2 copy-start.39
  56.6 5.9 copy-start.63
  60.5 10.5 %copy-start.75 = (f32[128]{0:T(128)}, f32[128]{0:T(128)S(1)}, u32[]{:S(2)}) copy-start(f32[128]{0:T(128)S(1)} %fusion.146) | copy-start | bytes 1540
  71.1 47.1 %copy-start.7 = (f32[128,2,1,64]{0,3,1,2:T(8,128)}, f32[128,2,1,64]{0,3,1,2:T(8,128)S(1)}, u32[]{:S(2)}) copy-start(f32[128,2,1,64]{0,3,1,2:T(8,128)S(1)} %copy.347) | copy-start | bytes 196612
  72.7 10.6 %copy-start.71 = (f32[128]{0:T(128)}, f32[128]{0:T(128)S(1)}, u32[]{:S(2)}) copy-start(f32[128]{0:T(128)S(1)} %fusion.147) | copy-start | bytes 1540
  83.3 44.7 %copy-start.5 = (f32[128,2,1,64]{0,3,1,2:T(8,128)}, f32[128,2,1,64]{0,3,1,2:T(8,128)S(1)}, u32[]{:S(2)}) copy-start(f32[128,2,1,64]{0,3,1,2:T(8,128)S(1)} %copy.368) | copy-start | bytes 196612
  83.4 34.8 %copy-start.76 = (f32[128]{0:T(128)S(1)}, f32[128]{0:T(128)}, u32[]{:S(2)}) copy-start(f32[128]{0:T(128)} %copy-done.75) | copy-start | bytes 1540
  119.4 6.1 copy-start.69
  128.0 5.2 copy-start.11
  128.1 5.1 copy-start.44
  128.7 5.2 copy-start.23
  129.3 4.6 copy-start.70
  134.7 9.7 %copy-start.77 = (f32[128]{0:T(128)S(1)}, f32[128]{0:T(128)}, u32[]{:S(2)}) copy-start(f32[128]{0:T(128)} %copy-done.75) | copy-start | bytes 1540
  134.7 10.6 %copy-start.18 = (f32[1,2,64,640]{3,2,1,0:T(8,128)S(1)}, f32[1,2,64,640]{3,2,1,0:T(8,128)}, u32[]{:S(2)}) copy-start(f32[1,2,64,640]{3,2,1,0:T(8,128)} %convolution_bitcast_fusion.2) | copy-start | bytes 983044
  134.7 10.6 %copy-start.21 = (f32[1,2,64,640]{3,2,1,0:T(8,128)S(1)}, f32[1,2,64,640]{3,2,1,0:T(8,128)}, u32[]{:S(2)}) copy-start(f32[1,2,64,640]{3,2,1,0:T(8,128)} %convolution_bitcast_fusion.3) | copy-start | bytes 983044
  148.7 9.8 %copy-start.35 = (f32[128,2,64]{2,1,0:T(2,128)S(1)}, f32[128,2,64]{2,1,0:T(2,128)}, u32[]{:S(2)}) copy-start(f32[128,2,64]{2,1,0:T(2,128)} %copy-done.32) | copy-start | bytes 196612
  148.7 9.8 %copy-start.40 = (f32[128,2,64]{2,1,0:T(2,128)S(1)}, f32[128,2,64]{2,1,0:T(2,128)}, u32[]{:S(2)}) copy-start(f32[128,2,64]{2,1,0:T(2,128)} %copy-done.37) | copy-start | bytes 196612
  148.7 9.7 %copy-start.48 = (f32[128,2,64]{2,1,0:T(2,128)S(1)}, f32[128,2,64]{2,1,0:T(2,128)}, u32[]{:S(2)}) copy-start(f32[128,2,64]{2,1,0:T(2,128)} %copy.408) | copy-start | bytes 196612
  148.7 9.7 %copy-start.50 = (f32[128,2,64]{2,1,0:T(2,128)S(1)}, f32[128,2,64]{2,1,0:T(2,128)}, u32[]{:S(2)}) copy-start(f32[128,2,64]{2,1,0:T(2,128)} %copy.410) | copy-start | bytes 196612
  148.7 9.7 %copy-start.60 = (f32[128,2,64]{0,2,1:T(8,128)S(1)}, f32[128,2,64]{0,2,1:T(8,128)}, u32[]{:S(2)}) copy-start(f32[128,2,64]{0,2,1:T(8,128)} %copy-done.57) | copy-start | bytes 196612
  148.7 9.7 %copy-start.64 = (f32[128,2,64]{0,2,1:T(8,128)S(1)}, f32[128,2,64]{0,2,1:T(8,128)}, u32[]{:S(2)}) copy-start(f32[128,2,64]{0,2,1:T(8,128)} %copy-done.62) | copy-start | bytes 196612
  148.7 9.7 %copy-start.67 = (pred[128,128]{1,0:T(8,128)(4,1)S(1)}, pred[128,128]{1,0:T(8,128)(4,1)}, u32[]{:S(2)}) copy-start(pred[128,128]{1,0:T(8,128)(4,1)} %copy-done.66) | copy-start | bytes 49156
  158.5 14.5 %copy-start.4 = (bf16[1,1,1,128,1280]{3,4,2,1,0:T(8,128)(2,1)S(1)}, bf16[1,1,1,128,1280]{3,4,2,1,0:T(8,128)(2,1)}, u32[]{:S(2)}) copy-start(bf16[1,1,1,128,1280]{3,4,2,1,0:T(8,128)(2,1)} %copy-done.3) | copy-start | bytes 983044
  175.3 19.7 %copy-start.8 = (f32[128,2,1,64]{0,3,1,2:T(8,128)S(1)}, f32[128,2,1,64]{0,3,1,2:T(8,128)}, u32[]{:S(2)}) copy-start(f32[128,2,1,64]{0,3,1,2:T(8,128)} %copy-done.7) | copy-start | bytes 196612
  175.3 19.7 %copy-start.10 = (f32[128,2,64]{0,2,1:T(8,128)S(1)}, f32[128,2,64]{0,2,1:T(8,128)}, u32[]{:S(2)}) copy-start(f32[128,2,64]{0,2,1:T(8,128)} %copy-done.9) | copy-start | bytes 196612
  175.3 19.7 %copy-start.26 = (f32[2,128,64]{1,2,0:T(8,128)S(1)}, f32[2,128,64]{1,2,0:T(8,128)}, u32[]{:S(2)}) copy-start(f32[2,128,64]{1,2,0:T(8,128)} %copy-done.25) | copy-start | bytes 196612
  175.4 19.7 %copy-start.29 = (f32[2,64,128]{2,1,0:T(8,128)S(1)}, f32[2,64,128]{2,1,0:T(8,128)}, u32[]{:S(2)}) copy-start(f32[2,64,128]{2,1,0:T(8,128)} %get-tuple-element.106) | copy-start | bytes 196612
  194.9 6.3 copy-start.6
  194.9 6.3 copy-start.12
  194.9 6.3 copy-start.24
  197.2 8.3 %copy-start.19 = (f32[1,2,64,640]{3,2,1,0:T(8,128)S(1)}, f32[1,2,64,640]{3,2,1,0:T(8,128)}, u32[]{:S(2)}) copy-start(f32[1,2,64,640]{3,2,1,0:T(8,128)} %convolution_bitcast_fusion.1) | copy-start | bytes 983044
  213.8 4.7 copy-start.55
  218.7 5.4 copy-start.74
  218.7 253.7 %all-to-all-start.1 = ((f32[32,2,2,2,2,640]{5,4,3,2,1,0:T(2,128)}), f32[32,2,2,2,2,640]{5,4,3,2,1,0:T(2,128)S(1)}, u32[]{:S(2)}, u32[]{:S(2)}) async-start(f32[32,2,2,2,2,640]{5,4,3,2,1,0:T(2,128)} %copy_bitcast_fusion), calls=%async_computation.1 | async-start | bytes 2621440 | tf_op jit(solution)/shard_map/all_to_all | solution.py:15
  224.0 428.4 %all-reduce.9.cloned.1.call-start = ((), (), s32[]{:S(2)}) async-start(), calls=%async_computation.4 | async-start | bytes 2621440 | tf_op jit(solution)/shard_map/psum | solution.py:118
  231.5 138.8 %copy-start.17 = (bf16[128,2,640]{0,2,1:T(8,128)(2,1)S(1)}, bf16[128,2,640]{0,2,1:T(8,128)(2,1)}, u32[]{:S(2)}) copy-start(bf16[128,2,640]{0,2,1:T(8,128)(2,1)} %copy.298) | copy-start | bytes 983044
  370.3 99.0 %copy-start.31 = (f32[128,128]{0,1:T(8,128)S(1)}, f32[128,128]{0,1:T(8,128)}, u32[]{:S(2)}) copy-start(f32[128,128]{0,1:T(8,128)} %copy-done.30) | copy-start | bytes 196612
  (37 other events, 119.9 us)
Sparse Core Ops, SparseCore 0:
  55.1 59.5 all-gather.1
  212.2 157.9 all-reduce.6
  372.8 279.4 all-reduce.8
